TPU v7x, 32 devices: a whole 2x2x4 slice. The times are simulated.
32 devices in a mesh: gx: 2 (over x), gy: 4 (over z), gz: 4 (over y, core).
Axes of the slice: x: 2, y: 2, z: 4, core: 2. Of those that a mesh axis runs over, the one named last changes fastest.
Arguments:
- fields: float32 [1, 64, 128, 512], P(None, 'gx', 'gy', 'gz'), may hold values from -13 to 13
- exponents: int32 [5], replicated, may hold values from -5 to -1
Outputs:
- coefficients: float32 [1, 64, 128, 512], P(None, 'gx', 'gy', 'gz')
- statistics: float32 [2, 1, 5], replicated
All inputs are finite; a program needn't handle non-finite values.
Results may differ from a plain program's by a relative error of at most 0.0003.
Values sent between devices are 32-bit elements; how exact they have to be, the bound alone decides.
A program may use at most 64 MiB of HBM per device.

v0:
```python
import jax
import jax.numpy as jnp
from jax import lax
from jax.sharding import PartitionSpec as P

FINE = 3
COARSE = 2


def shifted(block, axis, distance):
    devices = range(lax.axis_size(axis))
    route = [((i - distance) % len(devices), i) for i in devices]
    return lax.ppermute(block, axis, route)


def split_pair(values, axis_dim):
    length = values.shape[axis_dim]
    even_part = lax.slice_in_dim(values, 0, length, 2, axis_dim)
    odd_part = lax.slice_in_dim(values, 1, length, 2, axis_dim)
    return (even_part, odd_part)


def finish(values, even_part, detail, before_rim, axis_dim):
    half_length = detail.shape[axis_dim]
    behind = jnp.concatenate(
        (before_rim, lax.slice_in_dim(detail, 0, half_length - 1, 1, axis_dim)), axis_dim
    )
    smooth = even_part + 0.25 * (behind + detail)
    return jnp.stack((smooth, detail), axis_dim + 1).reshape(values.shape)


def lift_shifts(values, axis_dim, fetch_ahead, fetch_behind):
    even_part, odd_part = split_pair(values, axis_dim)
    half_length = even_part.shape[axis_dim]
    first_even = lax.slice_in_dim(even_part, 0, 1, 1, axis_dim)
    after_rim = fetch_ahead(first_even)
    ahead_even = jnp.concatenate(
        (lax.slice_in_dim(even_part, 1, half_length, 1, axis_dim), after_rim), axis_dim
    )
    detail = odd_part - 0.5 * (even_part + ahead_even)
    before_rim = fetch_behind(lax.slice_in_dim(detail, half_length - 1, half_length, 1, axis_dim))
    return finish(values, even_part, detail, before_rim, axis_dim)


def detail_mask(shape):
    parity_flags = [jnp.arange(shape[index_dim]) % 2 == 0 for index_dim in (1, 2, 3)]
    smooth_cells = (
        parity_flags[0][:, None, None]
        & parity_flags[1][None, :, None]
        & parity_flags[2][None, None, :]
    )
    return jnp.where(smooth_cells, 0.0, 1.0).astype(jnp.float32)[None]


def shrink(values, exponent):
    thresh = jnp.exp2(exponent.astype(jnp.float32))
    return jnp.sign(values) * jnp.maximum(jnp.abs(values) - thresh, 0.0)


def shards(fields, exponents):
    lifters = (
        lambda values: lift_shifts(
            values,
            1,
            lambda boundary: shifted(boundary, "gx", -1),
            lambda boundary: shifted(boundary, "gx", 1),
        ),
        lambda values: lift_shifts(
            values,
            2,
            lambda boundary: shifted(boundary, "gy", -1),
            lambda boundary: shifted(boundary, "gy", 1),
        ),
        lambda values: lift_shifts(
            values,
            3,
            lambda boundary: shifted(boundary, "gz", -1),
            lambda boundary: shifted(boundary, "gz", 1),
        ),
    )
    grid_x = lax.axis_size("gx")
    grid_y = lax.axis_size("gy")
    grid_z = lax.axis_size("gz")
    cell_total = fields.shape[1] * fields.shape[2] * fields.shape[3] * grid_x * grid_y * grid_z
    sharded_levels = FINE + COARSE
    current = fields
    layers = []
    energies = []
    retained = []
    for layer_index in range(sharded_levels):
        for lifter in lifters:
            current = lifter(current)
        masking = detail_mask(current.shape)
        shrunk = shrink(current, exponents[layer_index])
        level_count = 7.0 * cell_total / 8 ** (layer_index + 1)
        local_energy = jnp.sum(current * current * masking, axis=(1, 2, 3))
        local_kept = jnp.sum(jnp.abs(shrunk) * masking, axis=(1, 2, 3))
        summed_energy, summed_kept = lax.psum((local_energy, local_kept), ("gx", "gy", "gz"))
        energies.append(summed_energy / level_count)
        retained.append(summed_kept / level_count)
        layers.append(shrunk)
        current = current[:, ::2, ::2, ::2]
    result = current
    for shrunk in reversed(layers):
        result = shrunk.at[:, ::2, ::2, ::2].set(result)
    statistics = jnp.stack((jnp.stack(energies, 1), jnp.stack(retained, 1)))
    return (result, statistics)


def solution(mesh):
    placed = (P(None, "gx", "gy", "gz"), P())
    return jax.shard_map(
        shards,
        mesh=mesh,
        in_specs=placed,
        out_specs=(P(None, "gx", "gy", "gz"), P()),
        check_vma=False,
    )
```

profile of v0, /device:TPU:0, one launch (start us, length us, event | category | flops | bytes accessed | tf_op | source)
XLA Modules:
  0.0 298.5 jit_solution(10845907525781875963)
XLA Ops:
  1.7 3.0 %collective-permute-start = (f32[1,1,32,128]{3,2,1,0:T(8,128)S(1)}, f32[1,1,32,128]{3,2,1,0:T(8,128)S(1)}, u32[]{:S(2)}, u32[]{:S(2)}) collective-permute-start(f32[1,1,32,128]{3,2,1,0:T(8,128)S(1)} %slice.393), channel_id=1, source_target_pairs={{16,0},{0,16},{17,1},{1,17},{18,2},{2,18},{19,3},{3,19},{20,4},{4,... | collective-permute-start | bytes 49160 | tf_op jit(solution)/shard_map/ppermute | solution.py:13
  8.6 3.3 %collective-permute-done.1 = f32[1,1,32,128]{3,2,1,0:T(8,128)S(1)} collective-permute-done((f32[1,1,32,128]{3,2,1,0:T(8,128)S(1)}, f32[1,1,32,128]{3,2,1,0:T(8,128)S(1)}, u32[]{:S(2)}, u32[]{:S(2)}) %collective-permute-start.1) | collective-permute-done | bytes 16416 | tf_op jit(solution)/shard_map/ppermute | solution.py:13
  12.5 3.7 %collective-permute-start.2 = (f32[1,32,1,128]{3,2,1,0:T(1,128)S(1)}, f32[1,32,1,128]{3,2,1,0:T(1,128)S(1)}, u32[]{:S(2)}, u32[]{:S(2)}) collective-permute-start(f32[1,32,1,128]{3,2,1,0:T(1,128)S(1)} %slice.397), channel_id=1, source_target_pairs={{4,0},{8,4},{12,8},{0,12},{5,1},{9,5},{13,9},{1,13},{6,2},{10,6},{... | collective-permute-start | bytes 49160 | tf_op jit(solution)/shard_map/ppermute | solution.py:13
  18.7 4.9 %collective-permute-done.3 = f32[1,32,1,128]{3,2,1,0:T(1,128)S(1)} collective-permute-done((f32[1,32,1,128]{3,2,1,0:T(1,128)S(1)}, f32[1,32,1,128]{3,2,1,0:T(1,128)S(1)}, u32[]{:S(2)}, u32[]{:S(2)}) %collective-permute-start.3) | collective-permute-done | bytes 16416 | tf_op jit(solution)/shard_map/ppermute | solution.py:13
  23.8 10.7 %slice.293 = f32[1,32,32,64]{3,1,2,0:T(8,128)S(1)} slice(f32[1,32,32,128]{3,1,2,0:T(8,128)S(1)} %bitcast.129), slice={[0:1:1], [0:32:1], [0:32:1], [0:128:2]} | slice | bytes 524288 | tf_op jit(solution)/shard_map/slice | solution.py:18
  34.6 10.9 %slice.294 = f32[1,32,32,64]{3,1,2,0:T(8,128)S(1)} slice(f32[1,32,32,128]{3,1,2,0:T(8,128)S(1)} %bitcast.130), slice={[0:1:1], [0:32:1], [0:32:1], [1:128:2]} | slice | bytes 524288 | tf_op jit(solution)/shard_map/slice | solution.py:19
  47.3 7.5 %collective-permute-done.5 = f32[1,32,32,1]{3,1,2,0:T(8,128)S(1)} collective-permute-done((f32[1,32,32,1]{3,1,2,0:T(8,128)S(1)}, f32[1,32,32,1]{3,1,2,0:T(8,128)S(1)}, u32[]{:S(2)}, u32[]{:S(2)}) %collective-permute-start.5) | collective-permute-done | bytes 4128 | tf_op jit(solution)/shard_map/ppermute | solution.py:13
  55.0 1.5 fusion
  56.5 1.7 copy.174
  58.2 6.9 %slice.300 = f32[1,16,16,64]{2,1,3,0:T(8,128)S(1)} slice(f32[1,32,32,128]{2,1,3,0:T(8,128)S(1)} %bitcast.126), slice={[0:1:1], [0:32:2], [0:32:2], [0:128:2]} | slice | bytes 131072 | tf_op jit(solution)/shard_map/slice | solution.py:102
  66.7 2.9 collective-permute-done.6
  70.5 3.2 %collective-permute-done.7 = f32[1,1,16,64]{2,1,3,0:T(1,128)S(1)} collective-permute-done((f32[1,1,16,64]{2,1,3,0:T(1,128)S(1)}, f32[1,1,16,64]{2,1,3,0:T(1,128)S(1)}, u32[]{:S(2)}, u32[]{:S(2)}) %collective-permute-start.7) | collective-permute-done | bytes 4128 | tf_op jit(solution)/shard_map/ppermute | solution.py:13
  74.0 2.1 collective-permute-start.8
  76.2 1.5 collective-permute-done.8
  77.8 5.4 %collective-permute-done.9 = f32[1,16,1,64]{3,2,1,0:T(1,128)S(1)} collective-permute-done((f32[1,16,1,64]{3,2,1,0:T(1,128)S(1)}, f32[1,16,1,64]{3,2,1,0:T(1,128)S(1)}, u32[]{:S(2)}, u32[]{:S(2)}) %collective-permute-start.9) | collective-permute-done | bytes 4128 | tf_op jit(solution)/shard_map/ppermute | solution.py:13
  83.3 1.2 slice.313
  84.7 1.3 slice.314
  87.4 2.2 collective-permute-start.11
  90.3 1.9 collective-permute-done.11
  93.6 2.7 slice.320
  97.4 2.9 collective-permute-done.12
  101.0 3.1 %collective-permute-done.13 = f32[1,1,8,32]{2,1,3,0:T(1,128)S(1)} collective-permute-done((f32[1,1,8,32]{2,1,3,0:T(1,128)S(1)}, f32[1,1,8,32]{2,1,3,0:T(1,128)S(1)}, u32[]{:S(2)}, u32[]{:S(2)}) %collective-permute-start.13) | collective-permute-done | bytes 1056 | tf_op jit(solution)/shard_map/ppermute | solution.py:13
  104.3 2.1 collective-permute-start.14
  106.4 1.5 collective-permute-done.14
  108.9 4.6 %collective-permute-done.15 = f32[1,8,1,32]{3,2,1,0:T(1,128)S(1)} collective-permute-done((f32[1,8,1,32]{3,2,1,0:T(1,128)S(1)}, f32[1,8,1,32]{3,2,1,0:T(1,128)S(1)}, u32[]{:S(2)}, u32[]{:S(2)}) %collective-permute-start.15) | collective-permute-done | bytes 1056 | tf_op jit(solution)/shard_map/ppermute | solution.py:13
  114.2 1.2 collective-permute-done.16
  115.5 1.9 collective-permute-start.17
  121.7 1.3 copy.175
  123.0 1.1 collective-permute-done.18
  124.7 3.0 %collective-permute-done.19 = f32[1,1,4,16]{3,2,1,0:T(4,128)S(1)} collective-permute-done((f32[1,1,4,16]{3,2,1,0:T(4,128)S(1)}, f32[1,1,4,16]{3,2,1,0:T(4,128)S(1)}, u32[]{:S(2)}, u32[]{:S(2)}) %collective-permute-start.19) | collective-permute-done | bytes 288 | tf_op jit(solution)/shard_map/ppermute | solution.py:13
  127.8 2.1 collective-permute-start.20
  131.6 5.3 %collective-permute-done.21 = f32[1,4,1,16]{3,2,1,0:T(1,128)S(1)} collective-permute-done((f32[1,4,1,16]{3,2,1,0:T(1,128)S(1)}, f32[1,4,1,16]{3,2,1,0:T(1,128)S(1)}, u32[]{:S(2)}, u32[]{:S(2)}) %collective-permute-start.21) | collective-permute-done | bytes 288 | tf_op jit(solution)/shard_map/ppermute | solution.py:13
  137.3 1.3 collective-permute-done.22
  138.7 1.8 collective-permute-start.23
  140.6 1.2 collective-permute-done.23
  143.5 3.1 %collective-permute-done.24 = f32[1,1,2,8]{2,3,1,0:T(8,128)S(1)} collective-permute-done((f32[1,1,2,8]{2,3,1,0:T(8,128)S(1)}, f32[1,1,2,8]{2,3,1,0:T(8,128)S(1)}, u32[]{:S(2)}, u32[]{:S(2)}) %collective-permute-start.24) | collective-permute-done | bytes 96 | tf_op jit(solution)/shard_map/ppermute | solution.py:13
  147.2 3.0 %collective-permute-done.25 = f32[1,1,2,8]{2,3,1,0:T(8,128)S(1)} collective-permute-done((f32[1,1,2,8]{2,3,1,0:T(8,128)S(1)}, f32[1,1,2,8]{2,3,1,0:T(8,128)S(1)}, u32[]{:S(2)}, u32[]{:S(2)}) %collective-permute-start.25) | collective-permute-done | bytes 96 | tf_op jit(solution)/shard_map/ppermute | solution.py:13
  150.3 2.1 collective-permute-start.26
  152.4 1.5 collective-permute-done.26
  153.9 5.3 %collective-permute-done.27 = f32[1,2,1,8]{3,2,1,0:T(1,128)S(1)} collective-permute-done((f32[1,2,1,8]{3,2,1,0:T(1,128)S(1)}, f32[1,2,1,8]{3,2,1,0:T(1,128)S(1)}, u32[]{:S(2)}, u32[]{:S(2)}) %collective-permute-start.27) | collective-permute-done | bytes 96 | tf_op jit(solution)/shard_map/ppermute | solution.py:13
  159.5 1.3 collective-permute-done.28
  161.0 1.8 collective-permute-start.29
  162.8 1.2 collective-permute-done.29
  165.9 2.5 scatter_fusion.1
  168.4 15.1 %scatter_fusion.2 = f32[8,8,32]{2,1,0:T(8,128)S(1)} fusion(f32[8,8,32]{2,1,0:T(8,128)S(1)} %multiply_bitcast_fusion, s32[256]{0:T(256)S(1)} %reshape.1208, f32[256]{0:T(256)S(1)} %reshape.1210), kind=kCustom, calls=%fused_computation.2 | custom fusion | bytes 6144 | tf_op jit(solution)/shard_map/scatter | solution.py:105
  183.6 38.3 %all-reduce.1 = (f32[1]{0:T(128)}, f32[1]{0:T(128)}, f32[1]{0:T(128)}, f32[1]{0:T(128)}, f32[1]{0:T(128)}, /*index=5*/f32[1]{0:T(128)}, f32[1]{0:T(128)}, f32[1]{0:T(128)}, f32[1]{0:T(128)}, f32[1]{0:T(128)}) all-reduce(f32[1]{0:T(128)} %bitcast.68, f32[1]{0:T(128)} %bitcast.70, ...), channel_id=1, replica_groups=mesh['gx'=2,'gy'=4,'gz'=4] {'gx','gy','gz'}, use_global_device_ids=true, to_apply=%region_16.17 | all-reduce | flops 10 | bytes 80 | tf_op jit(solution)/shard_map/psum | solution.py:98
  229.0 8.1 %scatter_fusion.3 = f32[16384]{0:T(1024)S(1)} fusion(f32[16384]{0:T(1024)S(1)} %reshape.1216, s32[2048]{0:T(1024)S(1)} %reshape.1218, f32[2048]{0:T(1024)S(1)} %reshape.1220), kind=kCustom, calls=%fused_computation.3 | custom fusion | bytes 32768 | tf_op jit(solution)/shard_map/scatter | solution.py:105
  237.1 60.5 %scatter_fusion.4 = f32[131072]{0:T(1024)S(1)} fusion(f32[131072]{0:T(1024)S(1)} %bitcast.122, s32[16384]{0:T(1024)S(1)} %reshape.1228, f32[16384]{0:T(1024)S(1)} %scatter_fusion.3), kind=kCustom, calls=%fused_computation.4 | custom fusion | bytes 262144
  (219 shorter events, 30.8 us)
Async XLA Ops:
  0.6 7.0 %copy-start.3 = (s32[3]{0:T(128)S(1)}, s32[3]{0:T(128)}, u32[]{:S(2)}) copy-start(s32[3]{0:T(128)} %constant.207) | copy-start | bytes 40
  0.6 7.4 %copy-start.1 = (f32[1,32,32,128]{3,2,1,0:T(8,128)S(1)}, f32[1,32,32,128]{3,2,1,0:T(8,128)}, u32[]{:S(2)}) copy-start(f32[1,32,32,128]{3,2,1,0:T(8,128)} %param.2) | copy-start | bytes 1572868
  1.7 6.3 %collective-permute-start = (f32[1,1,32,128]{3,2,1,0:T(8,128)S(1)}, f32[1,1,32,128]{3,2,1,0:T(8,128)S(1)}, u32[]{:S(2)}, u32[]{:S(2)}) collective-permute-start(f32[1,1,32,128]{3,2,1,0:T(8,128)S(1)} %slice.393), channel_id=1, source_target_pairs={{16,0},{0,16},{17,1},{1,17},{18,2},{2,18},{19,3},{3,19},{20,4},{4,... | collective-permute-start | bytes 49160 | tf_op jit(solution)/shard_map/ppermute | solution.py:13
  8.1 3.8 %collective-permute-start.1 = (f32[1,1,32,128]{3,2,1,0:T(8,128)S(1)}, f32[1,1,32,128]{3,2,1,0:T(8,128)S(1)}, u32[]{:S(2)}, u32[]{:S(2)}) collective-permute-start(f32[1,1,32,128]{3,2,1,0:T(8,128)S(1)} %slice.394), channel_id=1, source_target_pairs={{16,0},{0,16},{17,1},{1,17},{18,2},{2,18},{19,3},{3,19},{20,4},{4,... | collective-permute-start | bytes 49160 | tf_op jit(solution)/shard_map/ppermute | solution.py:13
  12.0 6.0 %copy-start.2 = (s32[5]{0:T(128)S(1)}, s32[5]{0:T(128)}, u32[]{:S(2)}) copy-start(s32[5]{0:T(128)} %param.3) | copy-start | bytes 64
  12.5 5.1 %collective-permute-start.2 = (f32[1,32,1,128]{3,2,1,0:T(1,128)S(1)}, f32[1,32,1,128]{3,2,1,0:T(1,128)S(1)}, u32[]{:S(2)}, u32[]{:S(2)}) collective-permute-start(f32[1,32,1,128]{3,2,1,0:T(1,128)S(1)} %slice.397), channel_id=1, source_target_pairs={{4,0},{8,4},{12,8},{0,12},{5,1},{9,5},{13,9},{1,13},{6,2},{10,6},{... | collective-permute-start | bytes 49160 | tf_op jit(solution)/shard_map/ppermute | solution.py:13
  17.7 5.9 %collective-permute-start.3 = (f32[1,32,1,128]{3,2,1,0:T(1,128)S(1)}, f32[1,32,1,128]{3,2,1,0:T(1,128)S(1)}, u32[]{:S(2)}, u32[]{:S(2)}) collective-permute-start(f32[1,32,1,128]{3,2,1,0:T(1,128)S(1)} %slice.398), channel_id=1, source_target_pairs={{12,0},{0,4},{4,8},{8,12},{13,1},{1,5},{5,9},{9,13},{14,2},{2,6},{... | collective-permute-start | bytes 49160 | tf_op jit(solution)/shard_map/ppermute | solution.py:13
  34.5 11.1 %collective-permute-start.4 = (f32[1,32,32,1]{3,1,2,0:T(8,128)S(1)}, f32[1,32,32,1]{3,1,2,0:T(8,128)S(1)}, u32[]{:S(2)}, u32[]{:S(2)}) collective-permute-start(f32[1,32,32,1]{3,1,2,0:T(8,128)S(1)} %bitcast.128), channel_id=1, source_target_pairs={{1,0},{2,1},{3,2},{0,3},{5,4},{6,5},{7,6},{4,7},{9,8},{10,9},{11,1... | collective-permute-start | bytes 12296 | tf_op jit(solution)/shard_map/ppermute | solution.py:13
  46.1 8.7 %collective-permute-start.5 = (f32[1,32,32,1]{3,1,2,0:T(8,128)S(1)}, f32[1,32,32,1]{3,1,2,0:T(8,128)S(1)}, u32[]{:S(2)}, u32[]{:S(2)}) collective-permute-start(f32[1,32,32,1]{3,1,2,0:T(8,128)S(1)} %slice.402), channel_id=1, source_target_pairs={{3,0},{0,1},{1,2},{2,3},{7,4},{4,5},{5,6},{6,7},{11,8},{8,9},{9,10... | collective-permute-start | bytes 12296 | tf_op jit(solution)/shard_map/ppermute | solution.py:13
  65.6 4.0 %collective-permute-start.6 = (f32[1,1,16,64]{2,1,3,0:T(1,128)S(1)}, f32[1,1,16,64]{2,1,3,0:T(1,128)S(1)}, u32[]{:S(2)}, u32[]{:S(2)}) collective-permute-start(f32[1,1,16,64]{2,1,3,0:T(1,128)S(1)} %slice.405), channel_id=1, source_target_pairs={{16,0},{0,16},{17,1},{1,17},{18,2},{2,18},{19,3},{3,19},{20,4},{4,... | collective-permute-start | bytes 12296 | tf_op jit(solution)/shard_map/ppermute | solution.py:13
  69.7 4.0 %collective-permute-start.7 = (f32[1,1,16,64]{2,1,3,0:T(1,128)S(1)}, f32[1,1,16,64]{2,1,3,0:T(1,128)S(1)}, u32[]{:S(2)}, u32[]{:S(2)}) collective-permute-start(f32[1,1,16,64]{2,1,3,0:T(1,128)S(1)} %slice.406), channel_id=1, source_target_pairs={{16,0},{0,16},{17,1},{1,17},{18,2},{2,18},{19,3},{3,19},{20,4},{4,... | collective-permute-start | bytes 12296 | tf_op jit(solution)/shard_map/ppermute | solution.py:13
  74.0 3.7 %collective-permute-start.8 = (f32[1,16,1,64]{3,2,1,0:T(1,128)S(1)}, f32[1,16,1,64]{3,2,1,0:T(1,128)S(1)}, u32[]{:S(2)}, u32[]{:S(2)}) collective-permute-start(f32[1,16,1,64]{3,2,1,0:T(1,128)S(1)} %slice.409), channel_id=1, source_target_pairs={{4,0},{8,4},{12,8},{0,12},{5,1},{9,5},{13,9},{1,13},{6,2},{10,6},{... | collective-permute-start | bytes 12296 | tf_op jit(solution)/shard_map/ppermute | solution.py:13
  77.8 5.5 %collective-permute-start.9 = (f32[1,16,1,64]{3,2,1,0:T(1,128)S(1)}, f32[1,16,1,64]{3,2,1,0:T(1,128)S(1)}, u32[]{:S(2)}, u32[]{:S(2)}) collective-permute-start(f32[1,16,1,64]{3,2,1,0:T(1,128)S(1)} %slice.410), channel_id=1, source_target_pairs={{12,0},{0,4},{4,8},{8,12},{13,1},{1,5},{5,9},{9,13},{14,2},{2,6},{... | collective-permute-start | bytes 12296 | tf_op jit(solution)/shard_map/ppermute | solution.py:13
  84.6 2.6 collective-permute-start.10
  87.4 4.8 %collective-permute-start.11 = (f32[1,16,16,1]{3,1,2,0:T(8,128)S(1)}, f32[1,16,16,1]{3,1,2,0:T(8,128)S(1)}, u32[]{:S(2)}, u32[]{:S(2)}) collective-permute-start(f32[1,16,16,1]{3,1,2,0:T(8,128)S(1)} %slice.414), channel_id=1, source_target_pairs={{3,0},{0,1},{1,2},{2,3},{7,4},{4,5},{5,6},{6,7},{11,8},{8,9},{9,10... | collective-permute-start | bytes 3080 | tf_op jit(solution)/shard_map/ppermute | solution.py:13
  96.4 3.8 %collective-permute-start.12 = (f32[1,1,8,32]{2,1,3,0:T(1,128)S(1)}, f32[1,1,8,32]{2,1,3,0:T(1,128)S(1)}, u32[]{:S(2)}, u32[]{:S(2)}) collective-permute-start(f32[1,1,8,32]{2,1,3,0:T(1,128)S(1)} %slice.417), channel_id=1, source_target_pairs={{16,0},{0,16},{17,1},{1,17},{18,2},{2,18},{19,3},{3,19},{20,4},{4,... | collective-permute-start | bytes 3080 | tf_op jit(solution)/shard_map/ppermute | solution.py:13
  100.3 3.8 %collective-permute-start.13 = (f32[1,1,8,32]{2,1,3,0:T(1,128)S(1)}, f32[1,1,8,32]{2,1,3,0:T(1,128)S(1)}, u32[]{:S(2)}, u32[]{:S(2)}) collective-permute-start(f32[1,1,8,32]{2,1,3,0:T(1,128)S(1)} %slice.418), channel_id=1, source_target_pairs={{16,0},{0,16},{17,1},{1,17},{18,2},{2,18},{19,3},{3,19},{20,4},{4,... | collective-permute-start | bytes 3080 | tf_op jit(solution)/shard_map/ppermute | solution.py:13
  104.3 3.7 %collective-permute-start.14 = (f32[1,8,1,32]{3,2,1,0:T(1,128)S(1)}, f32[1,8,1,32]{3,2,1,0:T(1,128)S(1)}, u32[]{:S(2)}, u32[]{:S(2)}) collective-permute-start(f32[1,8,1,32]{3,2,1,0:T(1,128)S(1)} %slice.421), channel_id=1, source_target_pairs={{4,0},{8,4},{12,8},{0,12},{5,1},{9,5},{13,9},{1,13},{6,2},{10,6},{... | collective-permute-start | bytes 3080 | tf_op jit(solution)/shard_map/ppermute | solution.py:13
  108.0 5.5 %collective-permute-start.15 = (f32[1,8,1,32]{3,2,1,0:T(1,128)S(1)}, f32[1,8,1,32]{3,2,1,0:T(1,128)S(1)}, u32[]{:S(2)}, u32[]{:S(2)}) collective-permute-start(f32[1,8,1,32]{3,2,1,0:T(1,128)S(1)} %slice.422), channel_id=1, source_target_pairs={{12,0},{0,4},{4,8},{8,12},{13,1},{1,5},{5,9},{9,13},{14,2},{2,6},{... | collective-permute-start | bytes 3080 | tf_op jit(solution)/shard_map/ppermute | solution.py:13
  113.7 1.7 collective-permute-start.16
  115.5 3.3 %collective-permute-start.17 = (f32[1,8,8,1]{3,1,2,0:T(8,128)S(1)}, f32[1,8,8,1]{3,1,2,0:T(8,128)S(1)}, u32[]{:S(2)}, u32[]{:S(2)}) collective-permute-start(f32[1,8,8,1]{3,1,2,0:T(8,128)S(1)} %slice.426), channel_id=1, source_target_pairs={{3,0},{0,1},{1,2},{2,3},{7,4},{4,5},{5,6},{6,7},{11,8},{8,9},{9,10... | collective-permute-start | bytes 776 | tf_op jit(solution)/shard_map/ppermute | solution.py:13
  120.4 3.7 %collective-permute-start.18 = (f32[1,1,4,16]{3,2,1,0:T(4,128)S(1)}, f32[1,1,4,16]{3,2,1,0:T(4,128)S(1)}, u32[]{:S(2)}, u32[]{:S(2)}) collective-permute-start(f32[1,1,4,16]{3,2,1,0:T(4,128)S(1)} %get-tuple-element.34), channel_id=1, source_target_pairs={{16,0},{0,16},{17,1},{1,17},{18,2},{2,18},{19,3},{3,19},{20,4},{4,... | collective-permute-start | bytes 776 | tf_op jit(solution)/shard_map/ppermute | solution.py:13
  124.1 3.6 %collective-permute-start.19 = (f32[1,1,4,16]{3,2,1,0:T(4,128)S(1)}, f32[1,1,4,16]{3,2,1,0:T(4,128)S(1)}, u32[]{:S(2)}, u32[]{:S(2)}) collective-permute-start(f32[1,1,4,16]{3,2,1,0:T(4,128)S(1)} %get-tuple-element.31), channel_id=1, source_target_pairs={{16,0},{0,16},{17,1},{1,17},{18,2},{2,18},{19,3},{3,19},{20,4},{4,... | collective-permute-start | bytes 776 | tf_op jit(solution)/shard_map/ppermute | solution.py:13
  127.8 3.6 %collective-permute-start.20 = (f32[1,4,1,16]{3,2,1,0:T(1,128)S(1)}, f32[1,4,1,16]{3,2,1,0:T(1,128)S(1)}, u32[]{:S(2)}, u32[]{:S(2)}) collective-permute-start(f32[1,4,1,16]{3,2,1,0:T(1,128)S(1)} %get-tuple-element.30), channel_id=1, source_target_pairs={{4,0},{8,4},{12,8},{0,12},{5,1},{9,5},{13,9},{1,13},{6,2},{10,6},{... | collective-permute-start | bytes 776 | tf_op jit(solution)/shard_map/ppermute | solution.py:13
  131.5 5.4 %collective-permute-start.21 = (f32[1,4,1,16]{3,2,1,0:T(1,128)S(1)}, f32[1,4,1,16]{3,2,1,0:T(1,128)S(1)}, u32[]{:S(2)}, u32[]{:S(2)}) collective-permute-start(f32[1,4,1,16]{3,2,1,0:T(1,128)S(1)} %get-tuple-element.27), channel_id=1, source_target_pairs={{12,0},{0,4},{4,8},{8,12},{13,1},{1,5},{5,9},{9,13},{14,2},{2,6},{... | collective-permute-start | bytes 776 | tf_op jit(solution)/shard_map/ppermute | solution.py:13
  137.1 1.4 collective-permute-start.22
  138.7 3.1 %collective-permute-start.23 = (f32[1,4,4,1]{3,2,1,0:T(4,128)S(1)}, f32[1,4,4,1]{3,2,1,0:T(4,128)S(1)}, u32[]{:S(2)}, u32[]{:S(2)}) collective-permute-start(f32[1,4,4,1]{3,2,1,0:T(4,128)S(1)} %slice.438), channel_id=1, source_target_pairs={{3,0},{0,1},{1,2},{2,3},{7,4},{4,5},{5,6},{6,7},{11,8},{8,9},{9,10... | collective-permute-start | bytes 200 | tf_op jit(solution)/shard_map/ppermute | solution.py:13
  142.9 3.6 %collective-permute-start.24 = (f32[1,1,2,8]{2,3,1,0:T(8,128)S(1)}, f32[1,1,2,8]{2,3,1,0:T(8,128)S(1)}, u32[]{:S(2)}, u32[]{:S(2)}) collective-permute-start(f32[1,1,2,8]{2,3,1,0:T(8,128)S(1)} %slice.440), channel_id=1, source_target_pairs={{16,0},{0,16},{17,1},{1,17},{18,2},{2,18},{19,3},{3,19},{20,4},{4,... | collective-permute-start | bytes 200 | tf_op jit(solution)/shard_map/ppermute | solution.py:13
  146.5 3.6 %collective-permute-start.25 = (f32[1,1,2,8]{2,3,1,0:T(8,128)S(1)}, f32[1,1,2,8]{2,3,1,0:T(8,128)S(1)}, u32[]{:S(2)}, u32[]{:S(2)}) collective-permute-start(f32[1,1,2,8]{2,3,1,0:T(8,128)S(1)} %slice_subtract_fusion), channel_id=1, source_target_pairs={{16,0},{0,16},{17,1},{1,17},{18,2},{2,18},{19,3},{3,19},{20,4},{4,... | collective-permute-start | bytes 200 | tf_op jit(solution)/shard_map/ppermute | solution.py:13
  150.3 3.6 %collective-permute-start.26 = (f32[1,2,1,8]{3,2,1,0:T(1,128)S(1)}, f32[1,2,1,8]{3,2,1,0:T(1,128)S(1)}, u32[]{:S(2)}, u32[]{:S(2)}) collective-permute-start(f32[1,2,1,8]{3,2,1,0:T(1,128)S(1)} %slice.442), channel_id=1, source_target_pairs={{4,0},{8,4},{12,8},{0,12},{5,1},{9,5},{13,9},{1,13},{6,2},{10,6},{... | collective-permute-start | bytes 200 | tf_op jit(solution)/shard_map/ppermute | solution.py:13
  153.9 5.4 %collective-permute-start.27 = (f32[1,2,1,8]{3,2,1,0:T(1,128)S(1)}, f32[1,2,1,8]{3,2,1,0:T(1,128)S(1)}, u32[]{:S(2)}, u32[]{:S(2)}) collective-permute-start(f32[1,2,1,8]{3,2,1,0:T(1,128)S(1)} %slice_subtract_fusion.1), channel_id=1, source_target_pairs={{12,0},{0,4},{4,8},{8,12},{13,1},{1,5},{5,9},{9,13},{14,2},{2,6},{... | collective-permute-start | bytes 200 | tf_op jit(solution)/shard_map/ppermute | solution.py:13
  159.5 1.3 collective-permute-start.28
  161.0 3.0 %collective-permute-start.29 = (f32[1,2,2,1]{3,2,1,0:T(2,128)S(1)}, f32[1,2,2,1]{3,2,1,0:T(2,128)S(1)}, u32[]{:S(2)}, u32[]{:S(2)}) collective-permute-start(f32[1,2,2,1]{3,2,1,0:T(2,128)S(1)} %slice.446), channel_id=1, source_target_pairs={{3,0},{0,1},{1,2},{2,3},{7,4},{4,5},{5,6},{6,7},{11,8},{8,9},{9,10... | collective-permute-start | bytes 56 | tf_op jit(solution)/shard_map/ppermute | solution.py:13
  297.7 0.8 copy-start
where the time goes:
time: 299 us; the launch traced here: 298 us
  local copies, waits for them, and re-layouts  134 us (45%)
  waiting for transfers between devices  75 us (25%)
  blocking collectives  38.3 us (13%)
  starting transfers between devices  29.1 us (10%)
  between operations  11.2 us (4%)
  other arithmetic  10.7 us (4%)
    ppermute x30, waiting for transfers between devices, shifted(): return lax.ppermute(block, axis, route)  75 us
    unnamed x12, local copies, waits for them, and re-layouts  61.6 us
    psum x1, blocking collectives, shards(): lax.psum((local_energy, local_kept), ('gx', 'gy', 'gz'))  38.3 us
    ppermute x30, starting transfers between devices, shifted(): return lax.ppermute(block, axis, route)  29.1 us
    scatter x7, local copies, waits for them, and re-layouts, shards(): result = shrunk.at[:, ::2, ::2, ::2].set(result)  26.6 us
    slice x15, local copies, waits for them, and re-layouts, split_pair(): even_part = lax.slice_in_dim(values, 0, length, 2, axis_dim)  14.4 us
    slice x11, local copies, waits for them, and re-layouts, split_pair(): odd_part = lax.slice_in_dim(values, 1, length, 2, axis_dim)  13.4 us
    slice x5, local copies, waits for them, and re-layouts, shards(): current = current[:, ::2, ::2, ::2]  10.3 us
  transfers between devices with their start and end apart: 30, of which 28 were waited for; matrix products, arithmetic and copies ran while one was open for 7% of the time, Pallas kernels for 0%

commit v1 on v0

v1 whole, which is shorter than its diff:
```python
import functools

import numpy as np

import jax
import jax.numpy as jnp
from jax import lax
from jax.experimental import pallas as pl
from jax.experimental.pallas import tpu as pltpu
from jax.sharding import PartitionSpec as P

FINE = 3
LEVELS = 5
LANES = 128
MESH = pl.DeviceIdType.MESH


def periodic_lift(length):
    eye = np.eye(length)
    even, odd = eye[0::2], eye[1::2]
    detail = odd - 0.5 * (even + np.roll(even, -1, 0))
    smooth = even + 0.25 * (np.roll(detail, 1, 0) + detail)
    whole = np.zeros((length, length))
    whole[0::2] = smooth
    whole[1::2] = detail
    return whole


def second_lift(length):
    whole = np.zeros((length, length))
    whole[0::2, 0::2] = periodic_lift(length // 2)
    return whole


def coarse_matrices(sizes, coarse):
    nx, ny, nz = sizes
    cx, cy, cz = coarse
    rows = np.arange(nx * ny * cx * cy)
    dev, inner = rows // (cx * cy), rows % (cx * cy)
    gx = (dev // ny) * cx + inner // cy
    gy = (dev % ny) * cy + inner % cy
    step = LANES // cz
    lanes = np.array([z * step + d for d in range(nz) for z in range(cz)])
    result = []
    for make in (periodic_lift, second_lift):
        mx, my, mz = make(nx * cx), make(ny * cy), make(nz * cz)
        both = mx[gx[:, None], gx[None]] * my[gy[:, None], gy[None]]
        along = np.zeros((LANES, LANES))
        along[np.ix_(lanes, lanes)] = mz.T
        result += [both.astype(np.float32), along.astype(np.float32)]
    return result


def iota(shape, axis):
    return lax.broadcasted_iota(jnp.int32, shape, axis)


def roll(values, shift, axis):
    return pltpu.roll(values, shift % values.shape[axis], axis)


def lift_rows(v, low, high):
    n = v.shape[0]
    row = iota(v.shape, 0)
    odd = row % 2 == 1
    up = jnp.where(row == n - 1, high, roll(v, -1, 0))
    w = jnp.where(odd, v - 0.5 * (roll(v, 1, 0) + up), v)
    down = jnp.where(row == 0, low - 0.5 * v, roll(w, 1, 0))
    return jnp.where(odd, w, w + 0.25 * (down + roll(w, -1, 0)))


def lift_lanes(v, rim, s):
    lane = iota(v.shape, 1)
    up = jnp.where(lane == LANES - s, rim, roll(v, -s, 1))
    w = jnp.where(lane % (2 * s) == s, v - 0.5 * (roll(v, s, 1) + up), v)
    down = jnp.where(lane == 0, rim - 0.5 * v, roll(w, s, 1))
    return jnp.where(lane % (2 * s) == 0, w + 0.25 * (down + roll(w, -s, 1)), w)


def shrink(v, thresh):
    return v - jnp.clip(v, -thresh, thresh)


def kernel(sizes, cells, exps, field, k3, l3, k4, l4, out, stats, *scratch):
    nx, ny, nz = sizes
    ndev = nx * ny * nz
    scratch = list(scratch)
    me = (lax.axis_index("gx"), lax.axis_index("gy"), lax.axis_index("gz"))

    def device(dx, dy, dz):
        return (
            lax.rem(me[0] + (dx + nx), nx),
            lax.rem(me[1] + (dy + ny), ny),
            lax.rem(me[2] + (dz + nz), nz),
        )

    def thresh(level):
        return jnp.exp2(jnp.full((1, LANES), exps[level].astype(jnp.float32)))

    def split(j):
        return j // (ny * nz), (j // nz) % ny, j % nz

    barrier = pltpu.get_barrier_semaphore()

    def greet(j, carry):
        pl.semaphore_signal(barrier, inc=1, device_id=device(*split(j)), device_id_type=MESH)
        return carry

    lax.fori_loop(1, ndev, greet, 0)
    gath, msg, rows_s, final_s, g_send, g_recv = scratch[-6:]
    sums = []

    for level in range(FINE):
        (xs, xr, ys, yr, es, er, yl, zs, zr, work, nxt, xy_send, xy_recv, z_send, z_recv) = scratch[
            level * 15 : level * 15 + 15
        ]
        s = 2**level
        n = field.shape[2] // s
        px = field.shape[1] // s
        src = field.at[0] if level == 0 else scratch[(level - 1) * 15 + 10]

        e_plane = src[0]
        p_plane = src[px - 1] - 0.5 * src[px - 2]
        xs[0] = e_plane
        xs[1] = p_plane
        ys[0] = src[:, 0, :]
        ys[1] = src[:, n - 1, :] - 0.5 * src[:, n - 2, :]
        for a, plane in ((0, e_plane), (1, p_plane)):
            es[2 * a] = plane[0:1]
            es[2 * a + 1] = plane[n - 1 : n] - 0.5 * plane[n - 2 : n - 1]
        if level == 0:
            pl.semaphore_wait(barrier, ndev - 1)
        away = (-1, 1)
        copies = []
        for i, (a, b) in enumerate(((0, 0), (0, 1), (1, 0), (1, 1))):
            copies.append((es.at[2 * a + b], er.at[2 * a + b], (away[a], away[b], 0)))
        for b in (0, 1):
            copies.append((ys.at[b], yr.at[b], (0, away[b], 0)))
        for a in (0, 1):
            copies.append((xs.at[a], xr.at[a], (away[a], 0, 0)))
        flights = [
            pltpu.make_async_remote_copy(
                src_ref=f, dst_ref=t, send_sem=xy_send.at[i], recv_sem=xy_recv.at[i],
                device_id=device(*d), device_id_type=MESH,
            )
            for i, (f, t, d) in enumerate(copies)
        ]
        for flight in flights:
            flight.start()
        for flight in flights:
            flight.wait()

        for b in (0, 1):
            yl[b] = lift_rows(yr[b], er[2 + b], er[b])

        lane = iota((n, LANES), 1)

        def slot(x):
            return (x // s) * (2 * s) + x % s

        def plane_step(x, v, packed):
            v = lift_rows(v, yl[1, pl.ds(x, 1), :], yl[0, pl.ds(x, 1), :])
            work[x] = v
            u = jnp.where(lane == LANES - s, v - 0.5 * roll(v, s, 1), v)
            a = slot(x)
            mine = (lane == a) | (lane == a + s)
            return jnp.where(mine, pltpu.roll(u, lax.rem(a + s, LANES), 1), packed)

        def pair_step(k, even, after, before, packed):
            detail = src[2 * k + 1] - 0.5 * (even + after)
            smooth = even + 0.25 * (before + detail)
            packed = plane_step(2 * k, smooth, packed)
            packed = plane_step(2 * k + 1, detail, packed)
            return detail, packed

        def pair_loop(k, carry):
            even, before, packed = carry
            after = src[2 * k + 2]
            detail, packed = pair_step(k, even, after, before, packed)
            return after, detail, packed

        first = src[0]
        carry = (first, xr[1] - 0.5 * first, jnp.zeros((n, LANES), jnp.float32))
        even, before, packed = lax.fori_loop(0, px // 2 - 1, pair_loop, carry, unroll=3)
        _, packed = pair_step(px // 2 - 1, even, xr[0], before, packed)
        zs[...] = packed
        flights = [
            pltpu.make_async_remote_copy(
                src_ref=zs, dst_ref=zr.at[i], send_sem=z_send.at[i], recv_sem=z_recv.at[i],
                device_id=device(0, 0, away[i]), device_id_type=MESH,
            )
            for i in (0, 1)
        ]
        for flight in flights:
            flight.start()
        for flight in flights:
            flight.wait()
        rim = jnp.where(lane % (2 * s) < s, roll(zr[0], -s, 1), roll(zr[1], s, 1))
        level_thresh = thresh(level)
        inner = (lane % (2 * s) == 0) & (iota((n, LANES), 0) % 2 == 0)
        active = lane % s == 0

        def z_step(x, energy, kept, is_even):
            h = pltpu.roll(rim, LANES - s - slot(x), 1)
            v = lift_lanes(work[x], h, s)
            small = shrink(v, level_thresh)
            use = active & ~inner if is_even else active
            energy += jnp.where(use, v * v, 0.0)
            kept += jnp.where(use, jnp.abs(small), 0.0)
            if level == 0:
                out[0, x] = small
            else:
                spot = (0, s * x, pl.ds(0, n, stride=s), slice(None))
                out[spot] = jnp.where(active, small, out[spot])
            return v, energy, kept

        def z_loop(k, carry):
            energy, kept = carry
            v, energy, kept = z_step(2 * k, energy, kept, True)
            work[2 * k] = v
            nxt[k] = work[2 * k, pl.ds(0, n // 2, stride=2), :]
            _, energy, kept = z_step(2 * k + 1, energy, kept, False)
            return energy, kept

        zero = jnp.zeros((n, LANES), jnp.float32)
        energy, kept = lax.fori_loop(0, px // 2, z_loop, (zero, zero), unroll=2)
        sums += [energy, kept]

    last = scratch[(FINE - 1) * 15 + 10]
    cx, cy = last.shape[0], last.shape[1]
    step = 2**FINE
    count = cx * cy
    for x in range(cx):
        rows_s[pl.ds(x * cy, cy), :] = last[x]
    here = rows_s[...]
    lane = iota((count, LANES), 1)
    row = iota((count, LANES), 0)
    here = jnp.where(lane % step == 0, here, 0.0)
    for bit in (1, 2, 4):
        here = jnp.where((row & bit) != 0, roll(here, bit, 1), here)
    groups = count // 8
    one = iota((1, LANES), 1)
    for g in range(groups):
        msg[g : g + 1] = jnp.sum(here[8 * g : 8 * g + 8], axis=0, keepdims=True)
    tail = jnp.zeros((1, LANES), jnp.float32)
    for i, total in enumerate(sums):
        whole = jnp.sum(jnp.sum(total, axis=0, keepdims=True), axis=1, keepdims=True)
        tail = jnp.where(one == i, whole, tail)
    msg[groups:] = jnp.broadcast_to(tail, (msg.shape[0] - groups, LANES))
    flat = (me[0] * ny + me[1]) * nz + me[2]

    def post(j):
        return pltpu.make_async_remote_copy(
            src_ref=msg, dst_ref=gath.at[flat], send_sem=g_send.at[j], recv_sem=g_recv.at[j],
            device_id=device(*split(j)), device_id_type=MESH,
        )

    def send(j, carry):
        post(ndev - j).start()
        return carry

    def settle(j, carry):
        post(j).wait()
        return carry

    lax.fori_loop(1, ndev, send, 0)
    gath[flat] = msg[...]
    lax.fori_loop(1, ndev, settle, 0)

    sub = iota((8, LANES), 0)
    lane8 = iota((8, LANES), 1)

    def unpack(d, tail):
        for g in range(groups):
            acc = jnp.zeros((8, LANES), jnp.float32)
            for z in range(nz):
                v = jnp.broadcast_to(gath[d * nz + z, g : g + 1, :], (8, LANES))
                for bit in (1, 2, 4):
                    v = jnp.where((sub & bit) != 0, roll(v, -bit, 1), v)
                acc += roll(jnp.where(lane8 % step == 0, v, 0.0), z, 1)
            final_s[pl.ds(pl.multiple_of(d * count + 8 * g, 8), 8), :] = acc
        for z in range(nz):
            tail += gath[d * nz + z, groups : groups + 1, :]
        return tail

    tail = lax.fori_loop(0, nx * ny, unpack, jnp.zeros((1, LANES), jnp.float32))

    def dot(a, b):
        return jnp.dot(a, b, precision=lax.Precision.HIGHEST, preferred_element_type=jnp.float32)

    grid = final_s[...]
    grid = dot(dot(k3[...], grid), l3[...])
    grid4 = dot(dot(k4[...], grid), l4[...])
    row = iota(grid.shape, 0)
    lane = iota(grid.shape, 1)
    inner_row = row % count
    gx, gy, gz = inner_row // cy, inner_row % cy, lane // step
    valid = lane % step < nz
    even3 = (gx % 2 == 0) & (gy % 2 == 0) & (gz % 2 == 0)
    even4 = (gx % 4 == 0) & (gy % 4 == 0) & (gz % 4 == 0)
    det3 = valid & ~even3
    det4 = valid & even3 & ~even4
    small3 = shrink(grid, thresh(FINE))
    small4 = shrink(grid4, thresh(FINE + 1))
    final_s[...] = jnp.where(even3, jnp.where(even4, grid4, small4), small3)

    def total(mask, v):
        return jnp.sum(jnp.sum(jnp.where(mask, v, 0.0), axis=0, keepdims=True), axis=1, keepdims=True)

    coarse = ((total(det3, grid * grid), total(det3, jnp.abs(small3))),
              (total(det4, grid4 * grid4), total(det4, jnp.abs(small4))))
    for q in (0, 1):
        line = jnp.zeros((1, LANES), jnp.float32)
        for level in range(LEVELS):
            weight = 8.0 ** (level + 1) / (7.0 * cells)
            if level < FINE:
                value = jnp.sum(jnp.where(one == 2 * level + q, tail, 0.0), axis=1, keepdims=True)
            else:
                value = coarse[level - FINE][q]
            line = jnp.where(one == level, value * weight, line)
        stats[q] = line[:, 0:LEVELS]

    first = pl.multiple_of((me[0] * ny + me[1]) * count, count)
    mine = pltpu.roll(final_s[pl.ds(first, count), :], lax.rem(LANES - me[2], LANES), 1)
    rows_s[...] = mine
    keep = iota((cy, LANES), 1) % step == 0
    for x in range(cx):
        spot = (0, step * x, pl.ds(0, cy, stride=step), slice(None))
        out[spot] = jnp.where(keep, rows_s[pl.ds(x * cy, cy), :], out[spot])


def shards(sizes, fields, exponents):
    nx, ny, nz = sizes
    ndev = nx * ny * nz
    _, lx, ly, lz = fields.shape
    cells = fields.size * ndev
    step = 2**FINE
    coarse = (lx // step, ly // step, lz // step)
    count = coarse[0] * coarse[1]
    tables = coarse_matrices(sizes, coarse)
    scratch = []
    for level in range(FINE):
        x, y = lx >> level, ly >> level
        scratch += [
            pltpu.VMEM((2, y, LANES), jnp.float32),
            pltpu.VMEM((2, y, LANES), jnp.float32),
            pltpu.VMEM((2, x, LANES), jnp.float32),
            pltpu.VMEM((2, x, LANES), jnp.float32),
            pltpu.VMEM((4, 1, LANES), jnp.float32),
            pltpu.VMEM((4, 1, LANES), jnp.float32),
            pltpu.VMEM((2, x, LANES), jnp.float32),
            pltpu.VMEM((y, LANES), jnp.float32),
            pltpu.VMEM((2, y, LANES), jnp.float32),
            pltpu.VMEM((x, y, LANES), jnp.float32),
            pltpu.VMEM((x // 2, y // 2, LANES), jnp.float32),
            pltpu.SemaphoreType.DMA((8,)),
            pltpu.SemaphoreType.DMA((8,)),
            pltpu.SemaphoreType.DMA((2,)),
            pltpu.SemaphoreType.DMA((2,)),
        ]
    height = -(-(count // 8 + 1) // 4) * 4
    scratch += [
        pltpu.VMEM((ndev, height, LANES), jnp.float32),
        pltpu.VMEM((height, LANES), jnp.float32),
        pltpu.VMEM((count, LANES), jnp.float32),
        pltpu.VMEM((nx * ny * count, LANES), jnp.float32),
        pltpu.SemaphoreType.DMA((ndev,)),
        pltpu.SemaphoreType.DMA((ndev,)),
    ]
    vmem = pl.BlockSpec(memory_space=pltpu.VMEM)
    return pl.pallas_call(
        functools.partial(kernel, sizes, cells),
        out_shape=(
            jax.ShapeDtypeStruct(fields.shape, jnp.float32),
            jax.ShapeDtypeStruct((2, 1, LEVELS), jnp.float32),
        ),
        in_specs=[pl.BlockSpec(memory_space=pltpu.SMEM)] + [vmem] * 5,
        out_specs=(vmem, vmem),
        scratch_shapes=scratch,
        compiler_params=pltpu.CompilerParams(
            collective_id=0, has_side_effects=True, vmem_limit_bytes=48 * 2**20
        ),
    )(exponents, fields, *tables)


def solution(mesh):
    sizes = tuple(mesh.shape[name] for name in ("gx", "gy", "gz"))
    placed = (P(None, "gx", "gy", "gz"), P())
    return jax.shard_map(
        functools.partial(shards, sizes),
        mesh=mesh,
        in_specs=placed,
        out_specs=placed,
        check_vma=False,
    )
```

time: 299 us -> 47.4 us (0.16)
  local copies, waits for them, and re-layouts: 134 us -> 6.4 us
  waiting for transfers between devices: 75 us -> 0 us
  Pallas kernels: 0 us -> 40 us
  blocking collectives: 38.3 us -> 0 us
  starting transfers between devices: 29.1 us -> 0 us
  other arithmetic: 10.7 us -> 0 us
  between operations: 11.2 us -> 0.65 us
    ppermute x30 -> x0, waiting for transfers between devices: 75 us -> none  [shifted(): return lax.ppermute(block, axis, route)]
    unnamed x12 -> x14, local copies, waits for them, and re-layouts: 61.6 us -> 6.4 us
    slice x65 -> x0, local copies, waits for them, and re-layouts: 40 us -> none  [the longest x15 14.4 us: split_pair(): even_part = lax.slice_in_dim(values, 0, length, 2, axis_dim)]
    pallas_call x0 -> x1, Pallas kernels: none -> 40 us  [shards(): pl.pallas_call(functools.partial(kernel, sizes, cells), out_shape=(jax.Sh...]
    psum x1 -> x0, blocking collectives: 38.3 us -> none  [shards(): lax.psum((local_energy, local_kept), ('gx', 'gy', 'gz'))]
    ppermute x30 -> x0, starting transfers between devices: 29.1 us -> none  [shifted(): return lax.ppermute(block, axis, route)]
    scatter x7 -> x0, local copies, waits for them, and re-layouts: 26.6 us -> none  [shards(): result = shrunk.at[:, ::2, ::2, ::2].set(result)]
    reduce_sum x5 -> x0, other arithmetic: 4.56 us -> none  [shards(): local_energy = jnp.sum(current * current * masking, axis=(1, 2, 3))]
  transfers between devices with their start and end apart: 30 -> 0, of which waited for: 28 -> 0; matrix products, arithmetic and copies ran while one was open for 7% -> 0% of each run, Pallas kernels for 0% -> 0%
where the time goes in v1:
time: 47.4 us; the launch traced here: 47.1 us
  Pallas kernels  40 us (84%)
  local copies, waits for them, and re-layouts  6.4 us (14%)
  between operations  0.65 us (1%)
    pallas_call x1, Pallas kernels, shards(): pl.pallas_call(functools.partial(kernel, sizes, cells), out_shape=(jax.Sh...  40 us
    unnamed x14, local copies, waits for them, and re-layouts  6.4 us

profile of v1, /device:TPU:0, one launch (start us, length us, event | category | flops | bytes accessed | tf_op | source)
XLA Modules:
  0.0 47.1 jit_solution(14689724955098048594)
XLA Ops:
  0.6 0.0 copy-start
  0.6 1.0 %copy-done = f32[1,32,32,128]{3,2,1,0:T(8,128)S(1)} copy-done((f32[1,32,32,128]{3,2,1,0:T(8,128)S(1)}, f32[1,32,32,128]{3,2,1,0:T(8,128)}, u32[]{:S(2)}) %copy-start) | copy-done | bytes 524312
  1.7 0.0 copy-start.1
  1.7 0.8 %copy-done.1 = f32[128,128]{1,0:T(8,128)S(1)} copy-done((f32[128,128]{1,0:T(8,128)S(1)}, f32[128,128]{1,0:T(8,128)}, u32[]{:S(2)}) %copy-start.1) | copy-done | bytes 65560
  2.5 0.0 copy-start.2
  2.5 0.8 %copy-done.2 = f32[128,128]{1,0:T(8,128)S(1)} copy-done((f32[128,128]{1,0:T(8,128)S(1)}, f32[128,128]{1,0:T(8,128)}, u32[]{:S(2)}) %copy-start.2) | copy-done | bytes 65560
  3.4 0.0 copy-start.3
  3.4 0.8 %copy-done.3 = f32[128,128]{1,0:T(8,128)S(1)} copy-done((f32[128,128]{1,0:T(8,128)S(1)}, f32[128,128]{1,0:T(8,128)}, u32[]{:S(2)}) %copy-start.3) | copy-done | bytes 65560
  4.2 0.0 copy-start.4
  4.2 0.8 %copy-done.4 = f32[128,128]{1,0:T(8,128)S(1)} copy-done((f32[128,128]{1,0:T(8,128)S(1)}, f32[128,128]{1,0:T(8,128)}, u32[]{:S(2)}) %copy-start.4) | copy-done | bytes 65560
  5.0 0.0 copy-start.5
  5.0 0.7 %copy-done.5 = s32[5]{0:T(128)S(1)} copy-done((s32[5]{0:T(128)S(1)}, s32[5]{0:T(128)}, u32[]{:S(2)}) %copy-start.5) | copy-done | bytes 44
  5.7 40.0 %shard_map.77 = (f32[1,32,32,128]{3,2,1,0:T(8,128)S(1)}, f32[2,1,5]{2,1,0:T(1,128)S(1)}) custom-call(s32[5]{0:T(128)S(1)} %copy-done.5, f32[1,32,32,128]{3,2,1,0:T(8,128)S(1)} %copy-done, f32[128,128]{1,0:T(8,128)S(1)} %copy-done.4, f32[128,128]{1,0:T(8,128)S(1)} %copy-done.3, f32[128,128]{1,0:T(8,128)S(1)} %copy-done.2, f32[128,128]{1,0:T(8,128)S(1)} %copy-done.1), custom_call_target="tpu_custom_call" | custom-call | tf_op jit(solution)/shard_map/pallas_call | solution.py:371
  45.7 0.8 %copy.10 = f32[1,32,32,128]{3,2,1,0:T(8,128)} copy(f32[1,32,32,128]{3,2,1,0:T(8,128)S(1)} %get-tuple-element.4) | data formatting | bytes 1048576
  46.5 0.6 %copy.11 = f32[2,1,5]{2,1,0:T(1,128)} copy(f32[2,1,5]{2,1,0:T(1,128)S(1)} %get-tuple-element.5) | data formatting | bytes 80
Async XLA Ops:
  0.6 1.0 %copy-start = (f32[1,32,32,128]{3,2,1,0:T(8,128)S(1)}, f32[1,32,32,128]{3,2,1,0:T(8,128)}, u32[]{:S(2)}) copy-start(f32[1,32,32,128]{3,2,1,0:T(8,128)} %field.1) | copy-start | bytes 1572868
  1.7 0.8 %copy-start.1 = (f32[128,128]{1,0:T(8,128)S(1)}, f32[128,128]{1,0:T(8,128)}, u32[]{:S(2)}) copy-start(f32[128,128]{1,0:T(8,128)} %constant.11.clone.l4) | copy-start | bytes 196612
  2.5 0.8 %copy-start.2 = (f32[128,128]{1,0:T(8,128)S(1)}, f32[128,128]{1,0:T(8,128)}, u32[]{:S(2)}) copy-start(f32[128,128]{1,0:T(8,128)} %constant.10.clone.k4) | copy-start | bytes 196612
  3.4 0.8 %copy-start.3 = (f32[128,128]{1,0:T(8,128)S(1)}, f32[128,128]{1,0:T(8,128)}, u32[]{:S(2)}) copy-start(f32[128,128]{1,0:T(8,128)} %constant.9.clone.l3) | copy-start | bytes 196612
  4.2 0.8 %copy-start.4 = (f32[128,128]{1,0:T(8,128)S(1)}, f32[128,128]{1,0:T(8,128)}, u32[]{:S(2)}) copy-start(f32[128,128]{1,0:T(8,128)} %constant.8.clone.k3) | copy-start | bytes 196612
  5.0 0.7 %copy-start.5 = (s32[5]{0:T(128)S(1)}, s32[5]{0:T(128)}, u32[]{:S(2)}) copy-start(s32[5]{0:T(128)} %exps.1) | copy-start | bytes 64

commit v2 on v1

--- a/solution.py
+++ b/solution.py
@@ -12,6 +12,8 @@
 FINE = 3
 LEVELS = 5
 LANES = 128
+BUFFERS = 19
+VMEM_LIMIT = 67_043_328
 MESH = pl.DeviceIdType.MESH
 
 
@@ -47,8 +49,8 @@
         both = mx[gx[:, None], gx[None]] * my[gy[:, None], gy[None]]
         along = np.zeros((LANES, LANES))
         along[np.ix_(lanes, lanes)] = mz.T
-        result += [both.astype(np.float32), along.astype(np.float32)]
-    return result
+        result.append((both.astype(np.float32), along.astype(np.float32)))
+    return [np.stack(pair) for pair in zip(*result)]
 
 
 def iota(shape, axis):
@@ -81,10 +83,18 @@
     return v - jnp.clip(v, -thresh, thresh)
 
 
-def kernel(sizes, cells, exps, field, k3, l3, k4, l4, out, stats, *scratch):
+def kernel(sizes, cells, exps_in, field_in, rows_in, lanes_in, out, stats, *scratch):
     nx, ny, nz = sizes
     ndev = nx * ny * nz
     scratch = list(scratch)
+    field, exps, k_s, l_s, in_sem = scratch[-5:]
+    scratch = scratch[:-5]
+    loads = [
+        pltpu.make_async_copy(a, b, in_sem.at[i])
+        for i, (a, b) in enumerate(((field_in, field), (exps_in, exps), (rows_in, k_s), (lanes_in, l_s)))
+    ]
+    for load in loads:
+        load.start()
     me = (lax.axis_index("gx"), lax.axis_index("gy"), lax.axis_index("gz"))
 
     def device(dx, dy, dz):
@@ -102,22 +112,32 @@
 
     barrier = pltpu.get_barrier_semaphore()
 
-    def greet(j, carry):
-        pl.semaphore_signal(barrier, inc=1, device_id=device(*split(j)), device_id_type=MESH)
-        return carry
-
-    lax.fori_loop(1, ndev, greet, 0)
+    near = max(sizes) // 2 <= FINE
+    greeted = {
+        tuple((d + size - 1) % size if near else d for d, size in zip(spot, sizes))
+        for spot in np.ndindex(*(3, 3, 3) if near else sizes)
+    } - {(0, 0, 0)}
+    for spot in sorted(greeted):
+        pl.semaphore_signal(barrier, inc=1, device_id=device(*spot), device_id_type=MESH)
     gath, msg, rows_s, final_s, g_send, g_recv = scratch[-6:]
     sums = []
+    loads[0].wait()
+    loads[1].wait()
+    away = (-1, 1)
+    alone = nx == 2
 
     for level in range(FINE):
-        (xs, xr, ys, yr, es, er, yl, zs, zr, work, nxt, xy_send, xy_recv, z_send, z_recv) = scratch[
-            level * 15 : level * 15 + 15
+        (xs, xr, ys, yr, es, er, yl, zs, zr, hs, hr, ds, dr, cs, cr, work, nxt, send_sem, recv_sem) = scratch[
+            level * BUFFERS : level * BUFFERS + BUFFERS
         ]
         s = 2**level
         n = field.shape[2] // s
         px = field.shape[1] // s
-        src = field.at[0] if level == 0 else scratch[(level - 1) * 15 + 10]
+        src = field.at[0] if level == 0 else scratch[(level - 1) * BUFFERS + 16]
+        lane = iota((n, LANES), 1)
+
+        def edge(v):
+            return v[0:1], v[n - 1 : n] - 0.5 * v[n - 2 : n - 1]
 
         e_plane = src[0]
         p_plane = src[px - 1] - 0.5 * src[px - 2]
@@ -126,21 +146,46 @@
         ys[0] = src[:, 0, :]
         ys[1] = src[:, n - 1, :] - 0.5 * src[:, n - 2, :]
         for a, plane in ((0, e_plane), (1, p_plane)):
-            es[2 * a] = plane[0:1]
-            es[2 * a + 1] = plane[n - 1 : n] - 0.5 * plane[n - 2 : n - 1]
+            es[2 * a], es[2 * a + 1] = edge(plane)
+
+        packed = jnp.zeros((n, LANES), jnp.float32)
+        for x in range(px):
+            v = src[x]
+            u = jnp.where(lane == LANES - s, v - 0.5 * roll(v, s, 1), v)
+            at = 2 * s * x
+            packed = jnp.where((lane == at) | (lane == at + s), roll(u, at + s, 1), packed)
+        half = 2 * s * px
+        combined = packed - 0.5 * roll(packed, 2 * s, 1)
+        sides = roll(jnp.where(lane < half // 2, packed, combined), half, 1)
+        zs[...] = packed
+        hs[...] = sides
+        ds[0], ds[1] = edge(packed)
+        cs[0], cs[1] = edge(sides)
+
         if level == 0:
-            pl.semaphore_wait(barrier, ndev - 1)
-        away = (-1, 1)
+            pl.semaphore_wait(barrier, len(greeted))
         copies = []
-        for i, (a, b) in enumerate(((0, 0), (0, 1), (1, 0), (1, 1))):
-            copies.append((es.at[2 * a + b], er.at[2 * a + b], (away[a], away[b], 0)))
+        ways = (0,) if alone else (0, 1)
+        for i in (0, 1):
+            for b in (0, 1):
+                for a in ways:
+                    copies.append((cs.at[b], cr.at[4 * a + 2 * b + i], (away[a], away[b], away[i])))
+                copies.append((ds.at[b], dr.at[2 * b + i], (0, away[b], away[i])))
+        for a in (0, 1):
+            for b in (0, 1):
+                copies.append((es.at[2 * a + b], er.at[2 * a + b], (away[a], away[b], 0)))
         for b in (0, 1):
             copies.append((ys.at[b], yr.at[b], (0, away[b], 0)))
+        for i in (0, 1):
+            for a in ways:
+                copies.append((hs, hr.at[2 * a + i], (away[a], 0, away[i])))
         for a in (0, 1):
             copies.append((xs.at[a], xr.at[a], (away[a], 0, 0)))
+        for i in (0, 1):
+            copies.append((zs, zr.at[i], (0, 0, away[i])))
         flights = [
             pltpu.make_async_remote_copy(
-                src_ref=f, dst_ref=t, send_sem=xy_send.at[i], recv_sem=xy_recv.at[i],
+                src_ref=f, dst_ref=t, send_sem=send_sem.at[i], recv_sem=recv_sem.at[i],
                 device_id=device(*d), device_id_type=MESH,
             )
             for i, (f, t, d) in enumerate(copies)
@@ -153,58 +198,36 @@
         for b in (0, 1):
             yl[b] = lift_rows(yr[b], er[2 + b], er[b])
 
-        lane = iota((n, LANES), 1)
-
-        def slot(x):
-            return (x // s) * (2 * s) + x % s
-
-        def plane_step(x, v, packed):
-            v = lift_rows(v, yl[1, pl.ds(x, 1), :], yl[0, pl.ds(x, 1), :])
-            work[x] = v
-            u = jnp.where(lane == LANES - s, v - 0.5 * roll(v, s, 1), v)
-            a = slot(x)
-            mine = (lane == a) | (lane == a + s)
-            return jnp.where(mine, pltpu.roll(u, lax.rem(a + s, LANES), 1), packed)
-
-        def pair_step(k, even, after, before, packed):
-            detail = src[2 * k + 1] - 0.5 * (even + after)
-            smooth = even + 0.25 * (before + detail)
-            packed = plane_step(2 * k, smooth, packed)
-            packed = plane_step(2 * k + 1, detail, packed)
-            return detail, packed
-
-        def pair_loop(k, carry):
-            even, before, packed = carry
-            after = src[2 * k + 2]
-            detail, packed = pair_step(k, even, after, before, packed)
-            return after, detail, packed
-
-        first = src[0]
-        carry = (first, xr[1] - 0.5 * first, jnp.zeros((n, LANES), jnp.float32))
-        even, before, packed = lax.fori_loop(0, px // 2 - 1, pair_loop, carry, unroll=3)
-        _, packed = pair_step(px // 2 - 1, even, xr[0], before, packed)
-        zs[...] = packed
-        flights = [
-            pltpu.make_async_remote_copy(
-                src_ref=zs, dst_ref=zr.at[i], send_sem=z_send.at[i], recv_sem=z_recv.at[i],
-                device_id=device(0, 0, away[i]), device_id_type=MESH,
-            )
-            for i in (0, 1)
+        def rim_of(main, side):
+            spot = iota(main(0).shape, 1)
+            parts = []
+            for i in (0, 1):
+                after = side(0, i)
+                before = after if alone else side(1, i)
+                v = jnp.where(spot < half, main(i), 0.0)
+                v = jnp.where((spot >= half) & (spot < half + 2 * s), after, v)
+                parts.append(jnp.where(spot >= LANES - 2 * s, before, v))
+            v = jnp.where(spot % (2 * s) < s, roll(parts[0], -s, 1), roll(parts[1], s, 1))
+            odd = (spot // (2 * s)) % 2 == 1
+            w = jnp.where(odd, v - 0.5 * (roll(v, 2 * s, 1) + roll(v, -2 * s, 1)), v)
+            return jnp.where(odd, w, w + 0.25 * (roll(w, 2 * s, 1) + roll(w, -2 * s, 1)))
+
+        rim_rows = [
+            rim_of(lambda i: dr[2 * b + i], lambda a, i: cr[4 * a + 2 * b + i]) for b in (0, 1)
         ]
-        for flight in flights:
-            flight.start()
-        for flight in flights:
-            flight.wait()
-        rim = jnp.where(lane % (2 * s) < s, roll(zr[0], -s, 1), roll(zr[1], s, 1))
+        rim = rim_of(lambda i: zr[i], lambda a, i: hr[2 * a + i])
+        rim = lift_rows(rim, rim_rows[1], rim_rows[0])
         level_thresh = thresh(level)
         inner = (lane % (2 * s) == 0) & (iota((n, LANES), 0) % 2 == 0)
         active = lane % s == 0
 
-        def z_step(x, energy, kept, is_even):
-            h = pltpu.roll(rim, LANES - s - slot(x), 1)
-            v = lift_lanes(work[x], h, s)
+        energy = kept = jnp.zeros((n, LANES), jnp.float32)
+
+        def plane_step(x, v, energy, kept):
+            v = lift_rows(v, yl[1, x : x + 1, :], yl[0, x : x + 1, :])
+            v = lift_lanes(v, roll(rim, LANES - s - 2 * s * x, 1), s)
             small = shrink(v, level_thresh)
-            use = active & ~inner if is_even else active
+            use = active & ~inner if x % 2 == 0 else active
             energy += jnp.where(use, v * v, 0.0)
             kept += jnp.where(use, jnp.abs(small), 0.0)
             if level == 0:
@@ -212,21 +235,23 @@
             else:
                 spot = (0, s * x, pl.ds(0, n, stride=s), slice(None))
                 out[spot] = jnp.where(active, small, out[spot])
-            return v, energy, kept
-
-        def z_loop(k, carry):
-            energy, kept = carry
-            v, energy, kept = z_step(2 * k, energy, kept, True)
-            work[2 * k] = v
-            nxt[k] = work[2 * k, pl.ds(0, n // 2, stride=2), :]
-            _, energy, kept = z_step(2 * k + 1, energy, kept, False)
+            if x % 2 == 0:
+                work[x // 2] = v
+                nxt[x // 2] = work[x // 2, pl.ds(0, n // 2, stride=2), :]
             return energy, kept
 
-        zero = jnp.zeros((n, LANES), jnp.float32)
-        energy, kept = lax.fori_loop(0, px // 2, z_loop, (zero, zero), unroll=2)
+        even = src[0]
+        before = xr[1] - 0.5 * even
+        for k in range(px // 2):
+            after = src[2 * k + 2] if 2 * k + 2 < px else xr[0]
+            detail = src[2 * k + 1] - 0.5 * (even + after)
+            smooth = even + 0.25 * (before + detail)
+            energy, kept = plane_step(2 * k, smooth, energy, kept)
+            energy, kept = plane_step(2 * k + 1, detail, energy, kept)
+            even, before = after, detail
         sums += [energy, kept]
 
-    last = scratch[(FINE - 1) * 15 + 10]
+    last = scratch[(FINE - 1) * BUFFERS + 16]
     cx, cy = last.shape[0], last.shape[1]
     step = 2**FINE
     count = cx * cy
@@ -289,8 +314,10 @@
         return jnp.dot(a, b, precision=lax.Precision.HIGHEST, preferred_element_type=jnp.float32)
 
     grid = final_s[...]
-    grid = dot(dot(k3[...], grid), l3[...])
-    grid4 = dot(dot(k4[...], grid), l4[...])
+    loads[2].wait()
+    loads[3].wait()
+    grid = dot(dot(k_s[0], grid), l_s[0])
+    grid4 = dot(dot(k_s[1], grid), l_s[1])
     row = iota(grid.shape, 0)
     lane = iota(grid.shape, 1)
     inner_row = row % count
@@ -342,21 +369,13 @@
     for level in range(FINE):
         x, y = lx >> level, ly >> level
         scratch += [
-            pltpu.VMEM((2, y, LANES), jnp.float32),
-            pltpu.VMEM((2, y, LANES), jnp.float32),
-            pltpu.VMEM((2, x, LANES), jnp.float32),
-            pltpu.VMEM((2, x, LANES), jnp.float32),
-            pltpu.VMEM((4, 1, LANES), jnp.float32),
-            pltpu.VMEM((4, 1, LANES), jnp.float32),
-            pltpu.VMEM((2, x, LANES), jnp.float32),
-            pltpu.VMEM((y, LANES), jnp.float32),
-            pltpu.VMEM((2, y, LANES), jnp.float32),
-            pltpu.VMEM((x, y, LANES), jnp.float32),
-            pltpu.VMEM((x // 2, y // 2, LANES), jnp.float32),
-            pltpu.SemaphoreType.DMA((8,)),
-            pltpu.SemaphoreType.DMA((8,)),
-            pltpu.SemaphoreType.DMA((2,)),
-            pltpu.SemaphoreType.DMA((2,)),
+            *(pltpu.VMEM(shape, jnp.float32) for shape in (
+                (2, y, LANES), (2, y, LANES), (2, x, LANES), (2, x, LANES), (4, 1, LANES), (4, 1, LANES),
+                (2, x, LANES), (y, LANES), (2, y, LANES), (y, LANES), (4, y, LANES), (2, 1, LANES),
+                (4, 1, LANES), (2, 1, LANES), (8, 1, LANES), (x // 2, y, LANES), (x // 2, y // 2, LANES),
+            )),
+            pltpu.SemaphoreType.DMA((26,)),
+            pltpu.SemaphoreType.DMA((26,)),
         ]
     height = -(-(count // 8 + 1) // 4) * 4
     scratch += [
@@ -366,6 +385,11 @@
         pltpu.VMEM((nx * ny * count, LANES), jnp.float32),
         pltpu.SemaphoreType.DMA((ndev,)),
         pltpu.SemaphoreType.DMA((ndev,)),
+        pltpu.VMEM(fields.shape, jnp.float32),
+        pltpu.SMEM(exponents.shape, jnp.int32),
+        pltpu.VMEM(tables[0].shape, jnp.float32),
+        pltpu.VMEM(tables[1].shape, jnp.float32),
+        pltpu.SemaphoreType.DMA((4,)),
     ]
     vmem = pl.BlockSpec(memory_space=pltpu.VMEM)
     return pl.pallas_call(
@@ -374,11 +398,11 @@
             jax.ShapeDtypeStruct(fields.shape, jnp.float32),
             jax.ShapeDtypeStruct((2, 1, LEVELS), jnp.float32),
         ),
-        in_specs=[pl.BlockSpec(memory_space=pltpu.SMEM)] + [vmem] * 5,
+        in_specs=[pl.BlockSpec(memory_space=pltpu.HBM)] * 4,
         out_specs=(vmem, vmem),
         scratch_shapes=scratch,
         compiler_params=pltpu.CompilerParams(
-            collective_id=0, has_side_effects=True, vmem_limit_bytes=48 * 2**20
+            collective_id=0, has_side_effects=True, vmem_limit_bytes=VMEM_LIMIT
         ),
     )(exponents, fields, *tables)
 

time: 47.4 us -> 36 us (0.76)
  Pallas kernels: 40 us -> 32.8 us
  local copies, waits for them, and re-layouts: 6.4 us -> 2.44 us
    pallas_call x1, Pallas kernels: 40 us -> 32.8 us  [shards(): pl.pallas_call(functools.partial(kernel, sizes, cells), out_shape=(jax.Sh...]
    unnamed x14 -> x4, local copies, waits for them, and re-layouts: 6.4 us -> 2.44 us
where the time goes in v2:
time: 36 us; the launch traced here: 35.8 us
  Pallas kernels  32.8 us (91%)
  local copies, waits for them, and re-layouts  2.44 us (7%)
  between operations  0.65 us (2%)
    pallas_call x1, Pallas kernels, shards(): pl.pallas_call(functools.partial(kernel, sizes, cells), out_shape=(jax.Sh...  32.8 us
    unnamed x4, local copies, waits for them, and re-layouts  2.44 us

profile of v2, /device:TPU:0, one launch (start us, length us, event | category | flops | bytes accessed | tf_op | source)
XLA Modules:
  0.0 35.8 jit_solution(8824176843024528230)
XLA Ops:
  0.6 32.8 %shard_map.59 = (f32[1,32,32,128]{3,2,1,0:T(8,128)}, f32[2,1,5]{2,1,0:T(1,128)}) custom-call(s32[5]{0:T(128)} %exps_in.1, f32[1,32,32,128]{3,2,1,0:T(8,128)} %field_in.1, f32[2,128,128]{2,1,0:T(8,128)} %constant.4.clone.rows_in, f32[2,128,128]{2,1,0:T(8,128)} %constant.5.clone.lanes_in), custom_call_target="tpu_custom_call" | custom-call | tf_op jit(solution)/shard_map/pallas_call | solution.py:395
  33.4 0.0 copy-start
  33.4 1.9 %copy.8 = f32[1,32,32,128]{3,2,1,0:T(8,128)} copy(f32[1,32,32,128]{3,2,1,0:T(8,128)} %get-tuple-element.4) | data formatting | bytes 1048576
  35.3 0.0 copy-done
  35.3 0.6 %copy.9 = f32[2,1,5]{2,1,0:T(1,128)} copy(f32[2,1,5]{2,1,0:T(1,128)S(1)} %copy-done) | data formatting | bytes 80
Async XLA Ops:
  33.4 1.9 %copy-start = (f32[2,1,5]{2,1,0:T(1,128)S(1)}, f32[2,1,5]{2,1,0:T(1,128)}, u32[]{:S(2)}) copy-start(f32[2,1,5]{2,1,0:T(1,128)} %get-tuple-element.5) | copy-start | bytes 124

commit v3 on v2

--- a/solution.py
+++ b/solution.py
@@ -44,8 +44,10 @@
     step = LANES // cz
     lanes = np.array([z * step + d for d in range(nz) for z in range(cz)])
     result = []
-    for make in (periodic_lift, second_lift):
-        mx, my, mz = make(nx * cx), make(ny * cy), make(nz * cz)
+    for both_levels in (False, True):
+        mx, my, mz = periodic_lift(nx * cx), periodic_lift(ny * cy), periodic_lift(nz * cz)
+        if both_levels:
+            mx, my, mz = second_lift(nx * cx) @ mx, second_lift(ny * cy) @ my, second_lift(nz * cz) @ mz
         both = mx[gx[:, None], gx[None]] * my[gy[:, None], gy[None]]
         along = np.zeros((LANES, LANES))
         along[np.ix_(lanes, lanes)] = mz.T
@@ -288,9 +290,17 @@
         post(j).wait()
         return carry
 
-    lax.fori_loop(1, ndev, send, 0)
-    gath[flat] = msg[...]
-    lax.fori_loop(1, ndev, settle, 0)
+    if ndev <= 32:
+        posts = [post(ndev - j) for j in range(1, ndev)]
+        for flight in posts:
+            flight.start()
+        gath[flat] = msg[...]
+        for flight in posts:
+            flight.wait()
+    else:
+        lax.fori_loop(1, ndev, send, 0)
+        gath[flat] = msg[...]
+        lax.fori_loop(1, ndev, settle, 0)
 
     sub = iota((8, LANES), 0)
     lane8 = iota((8, LANES), 1)
@@ -308,7 +318,7 @@
             tail += gath[d * nz + z, groups : groups + 1, :]
         return tail
 
-    tail = lax.fori_loop(0, nx * ny, unpack, jnp.zeros((1, LANES), jnp.float32))
+    tail = lax.fori_loop(0, nx * ny, unpack, jnp.zeros((1, LANES), jnp.float32), unroll=nx * ny <= 8)
 
     def dot(a, b):
         return jnp.dot(a, b, precision=lax.Precision.HIGHEST, preferred_element_type=jnp.float32)
@@ -316,8 +326,8 @@
     grid = final_s[...]
     loads[2].wait()
     loads[3].wait()
-    grid = dot(dot(k_s[0], grid), l_s[0])
-    grid4 = dot(dot(k_s[1], grid), l_s[1])
+    half3, half4 = dot(k_s[0], grid), dot(k_s[1], grid)
+    grid, grid4 = dot(half3, l_s[0]), dot(half4, l_s[1])
     row = iota(grid.shape, 0)
     lane = iota(grid.shape, 1)
     inner_row = row % count

time: 36 us -> 33.9 us (0.942)
  Pallas kernels: 32.8 us -> 30.7 us
    pallas_call x1, Pallas kernels: 32.8 us -> 30.7 us  [shards(): pl.pallas_call(functools.partial(kernel, sizes, cells), out_shape=(jax.Sh...]
where the time goes in v3:
time: 33.9 us; the launch traced here: 33.7 us
  Pallas kernels  30.7 us (91%)
  local copies, waits for them, and re-layouts  2.44 us (7%)
  between operations  0.65 us (2%)
    pallas_call x1, Pallas kernels, shards(): pl.pallas_call(functools.partial(kernel, sizes, cells), out_shape=(jax.Sh...  30.7 us
    unnamed x4, local copies, waits for them, and re-layouts  2.44 us

profile of v3, /device:TPU:0, one launch (start us, length us, event | category | flops | bytes accessed | tf_op | source)
XLA Modules:
  0.0 33.7 jit_solution(9777971847346951145)
XLA Ops:
  0.6 30.7 %shard_map.59 = (f32[1,32,32,128]{3,2,1,0:T(8,128)}, f32[2,1,5]{2,1,0:T(1,128)}) custom-call(s32[5]{0:T(128)} %exps_in.1, f32[1,32,32,128]{3,2,1,0:T(8,128)} %field_in.1, f32[2,128,128]{2,1,0:T(8,128)} %constant.4.clone.rows_in, f32[2,128,128]{2,1,0:T(8,128)} %constant.5.clone.lanes_in), custom_call_target="tpu_custom_call" | custom-call | tf_op jit(solution)/shard_map/pallas_call | solution.py:405
  31.3 0.0 copy-start
  31.3 1.9 %copy.8 = f32[1,32,32,128]{3,2,1,0:T(8,128)} copy(f32[1,32,32,128]{3,2,1,0:T(8,128)} %get-tuple-element.4) | data formatting | bytes 1048576
  33.2 0.0 copy-done
  33.2 0.6 %copy.9 = f32[2,1,5]{2,1,0:T(1,128)} copy(f32[2,1,5]{2,1,0:T(1,128)S(1)} %copy-done) | data formatting | bytes 80
Async XLA Ops:
  31.3 1.9 %copy-start = (f32[2,1,5]{2,1,0:T(1,128)S(1)}, f32[2,1,5]{2,1,0:T(1,128)}, u32[]{:S(2)}) copy-start(f32[2,1,5]{2,1,0:T(1,128)} %get-tuple-element.5) | copy-start | bytes 124

commit v4 on v3

--- a/solution.py
+++ b/solution.py
@@ -194,6 +194,8 @@
         ]
         for flight in flights:
             flight.start()
+        if level > 0:
+            sums += finish()
         for flight in flights:
             flight.wait()
 
@@ -223,24 +225,29 @@
         inner = (lane % (2 * s) == 0) & (iota((n, LANES), 0) % 2 == 0)
         active = lane % s == 0
 
-        energy = kept = jnp.zeros((n, LANES), jnp.float32)
-
-        def plane_step(x, v, energy, kept):
+        def plane_step(x, v):
             v = lift_rows(v, yl[1, x : x + 1, :], yl[0, x : x + 1, :])
             v = lift_lanes(v, roll(rim, LANES - s - 2 * s * x, 1), s)
-            small = shrink(v, level_thresh)
-            use = active & ~inner if x % 2 == 0 else active
-            energy += jnp.where(use, v * v, 0.0)
-            kept += jnp.where(use, jnp.abs(small), 0.0)
-            if level == 0:
-                out[0, x] = small
-            else:
-                spot = (0, s * x, pl.ds(0, n, stride=s), slice(None))
-                out[spot] = jnp.where(active, small, out[spot])
+            work[x] = v
             if x % 2 == 0:
-                work[x // 2] = v
-                nxt[x // 2] = work[x // 2, pl.ds(0, n // 2, stride=2), :]
-            return energy, kept
+                nxt[x // 2] = work[x, pl.ds(0, n // 2, stride=2), :]
+
+        def finish(level=level, work=work, px=px, n=n, s=s, inner=inner, active=active, t=level_thresh):
+            energy = kept = jnp.zeros((n, LANES), jnp.float32)
+            for x in range(px):
+                v = work[x]
+                small = shrink(v, t)
+                use = active & ~inner if x % 2 == 0 else active
+                energy += jnp.where(use, v * v, 0.0)
+                kept += jnp.where(use, jnp.abs(small), 0.0)
+                if level == 0:
+                    out[0, x] = small
+                else:
+                    spot = (0, s * x, pl.ds(0, n, stride=s), slice(None))
+                    out[spot] = jnp.where(active, small, out[spot])
+            return [
+                jnp.sum(jnp.sum(v, axis=0, keepdims=True), axis=1, keepdims=True) for v in (energy, kept)
+            ]
 
         even = src[0]
         before = xr[1] - 0.5 * even
@@ -248,10 +255,9 @@
             after = src[2 * k + 2] if 2 * k + 2 < px else xr[0]
             detail = src[2 * k + 1] - 0.5 * (even + after)
             smooth = even + 0.25 * (before + detail)
-            energy, kept = plane_step(2 * k, smooth, energy, kept)
-            energy, kept = plane_step(2 * k + 1, detail, energy, kept)
+            plane_step(2 * k, smooth)
+            plane_step(2 * k + 1, detail)
             even, before = after, detail
-        sums += [energy, kept]
 
     last = scratch[(FINE - 1) * BUFFERS + 16]
     cx, cy = last.shape[0], last.shape[1]
@@ -270,8 +276,7 @@
     for g in range(groups):
         msg[g : g + 1] = jnp.sum(here[8 * g : 8 * g + 8], axis=0, keepdims=True)
     tail = jnp.zeros((1, LANES), jnp.float32)
-    for i, total in enumerate(sums):
-        whole = jnp.sum(jnp.sum(total, axis=0, keepdims=True), axis=1, keepdims=True)
+    for i, whole in enumerate(sums + finish()):
         tail = jnp.where(one == i, whole, tail)
     msg[groups:] = jnp.broadcast_to(tail, (msg.shape[0] - groups, LANES))
     flat = (me[0] * ny + me[1]) * nz + me[2]
@@ -382,7 +387,7 @@
             *(pltpu.VMEM(shape, jnp.float32) for shape in (
                 (2, y, LANES), (2, y, LANES), (2, x, LANES), (2, x, LANES), (4, 1, LANES), (4, 1, LANES),
                 (2, x, LANES), (y, LANES), (2, y, LANES), (y, LANES), (4, y, LANES), (2, 1, LANES),
-                (4, 1, LANES), (2, 1, LANES), (8, 1, LANES), (x // 2, y, LANES), (x // 2, y // 2, LANES),
+                (4, 1, LANES), (2, 1, LANES), (8, 1, LANES), (x, y, LANES), (x // 2, y // 2, LANES),
             )),
             pltpu.SemaphoreType.DMA((26,)),
             pltpu.SemaphoreType.DMA((26,)),

time: 33.9 us -> 33.5 us (0.988)
  Pallas kernels: 30.7 us -> 30.3 us
    pallas_call x1, Pallas kernels: 30.7 us -> 30.3 us  [shards(): pl.pallas_call(functools.partial(kernel, sizes, cells), out_shape=(jax.Sh...]
where the time goes in v4:
time: 33.5 us; the launch traced here: 33.4 us
  Pallas kernels  30.3 us (90%)
  local copies, waits for them, and re-layouts  2.44 us (7%)
  between operations  0.65 us (2%)
    pallas_call x1, Pallas kernels, shards(): pl.pallas_call(functools.partial(kernel, sizes, cells), out_shape=(jax.Sh...  30.3 us
    unnamed x4, local copies, waits for them, and re-layouts  2.44 us

profile of v4, /device:TPU:0, one launch (start us, length us, event | category | flops | bytes accessed | tf_op | source)
XLA Modules:
  0.0 33.4 jit_solution(7430399102834669188)
XLA Ops:
  0.6 30.3 %shard_map.59 = (f32[1,32,32,128]{3,2,1,0:T(8,128)}, f32[2,1,5]{2,1,0:T(1,128)}) custom-call(s32[5]{0:T(128)} %exps_in.1, f32[1,32,32,128]{3,2,1,0:T(8,128)} %field_in.1, f32[2,128,128]{2,1,0:T(8,128)} %constant.4.clone.rows_in, f32[2,128,128]{2,1,0:T(8,128)} %constant.5.clone.lanes_in), custom_call_target="tpu_custom_call" | custom-call | tf_op jit(solution)/shard_map/pallas_call | solution.py:410
  30.9 0.0 copy-start
  31.0 1.9 %copy.8 = f32[1,32,32,128]{3,2,1,0:T(8,128)} copy(f32[1,32,32,128]{3,2,1,0:T(8,128)} %get-tuple-element.4) | data formatting | bytes 1048576
  32.8 0.0 copy-done
  32.8 0.6 %copy.9 = f32[2,1,5]{2,1,0:T(1,128)} copy(f32[2,1,5]{2,1,0:T(1,128)S(1)} %copy-done) | data formatting | bytes 80
Async XLA Ops:
  30.9 1.9 %copy-start = (f32[2,1,5]{2,1,0:T(1,128)S(1)}, f32[2,1,5]{2,1,0:T(1,128)}, u32[]{:S(2)}) copy-start(f32[2,1,5]{2,1,0:T(1,128)} %get-tuple-element.5) | copy-start | bytes 124
